TPU v7x, 32 devices: a whole 2x2x4 slice. The times are simulated.
32 devices in a mesh: groups: 2 (over y), ctx: 4 (over z), head: 2 (over x), rep: 2 (over core).
Axes of the slice: x: 2, y: 2, z: 4, core: 2. Of those that a mesh axis runs over, the one named last changes fastest.
Arguments:
- queries: bfloat16 [2048, 4096], P(('groups', 'ctx'), ('head', 'rep')), parts along dimension 0, may hold values from -24 to 24
- keys: bfloat16 [2048, 1024], P(('groups', 'ctx'), ('head', 'rep')), parts along dimension 0, may hold values from -6 to 6
- values: bfloat16 [2048, 1024], P(('groups', 'ctx'), ('head', 'rep')), parts along dimension 0, may hold values from -6 to 6
- span_order: int32 [8], replicated, may hold values from 0 to 7, as said below
Outputs:
- attended: bfloat16 [2048, 4096], P(('groups', 'ctx'), ('head', 'rep')), parts along dimension 0
There are 2 independent parts, one for each index of `groups`. A program takes and returns all parts, laid end to end along the dimension named above; an argument that names none is the same for every part. Nothing has to cross between parts.
Inputs may be any that keep to these rules, and one draw needn't show every extreme that they name: `span_order`: A permutation of the spans in which entries 2 d and 2 d + 1 are c and 7 - c for some c.
All inputs are finite; a program needn't handle non-finite values.
Results may differ from a plain program's by a relative error of at most 0.0047.
Values may be sent and summed in bfloat16 or wider, within the bound.
A program may use at most 64 MiB of HBM per device.

v0:
```python
import math
import jax
import jax.numpy as jnp
from jax import lax
from jax.sharding import PartitionSpec as P

HEAD_SIZE = 128
masked_score = -1e30


def lookup_positions(span_order, first_row, row_count, span_rows):
    row_ids = first_row + jnp.arange(row_count, dtype=jnp.int32)
    span_ids = row_ids // span_rows
    span_table = jnp.arange(span_order.shape[0], dtype=jnp.int32)
    span_starts = jnp.sum(
        jnp.where(span_ids[:, None] == span_table[None, :], span_order[None, :], 0), axis=1
    )
    return span_starts * span_rows + row_ids % span_rows


def source_partials(query_block, query_pos, key_group, value_group, key_pos, head_dim):
    score_scale = 1.0 / math.sqrt(head_dim)
    scores = (
        jnp.einsum("rhgd,cshd->crhgs", query_block, key_group, preferred_element_type=jnp.float32)
        * score_scale
    )
    allowed = (key_pos[:, None, :] <= query_pos[None, :, None])[:, :, None, None, :]
    masked = jnp.where(allowed, scores, masked_score)
    row_top = jnp.max(masked, axis=-1)
    weights = jnp.where(allowed, jnp.exp(masked - row_top[..., None]), 0.0)
    row_total = jnp.sum(weights, axis=-1)
    numerator = jnp.einsum(
        "crhgs,cshd->crhgd",
        weights.astype(jnp.bfloat16),
        value_group,
        preferred_element_type=jnp.float32,
    )
    partial_value = (numerator / jnp.maximum(row_total, 1.0)[..., None]).astype(jnp.bfloat16)
    return (partial_value, row_top, row_total)


def absorb(running, partial_value, row_top, row_total):
    run_top, run_total, run_sum = running
    new_top = jnp.maximum(run_top, row_top)
    rescale = jnp.exp(run_top - new_top)
    source_weight = row_total * jnp.exp(row_top - new_top)
    return (
        new_top,
        run_total * rescale + source_weight,
        run_sum * rescale[..., None] + source_weight[..., None] * partial_value.astype(jnp.float32),
    )


def shards(queries, keys, values, span_order):
    rows_here = queries.shape[0]
    span_rows = rows_here // 2
    head_dim = HEAD_SIZE
    kv_heads = keys.shape[1] // head_dim
    common_values = queries.shape[1] // keys.shape[1]
    my_index = lax.axis_index("ctx")
    own_pos = lookup_positions(span_order, my_index * rows_here, rows_here, span_rows)
    q_local = queries.reshape(rows_here, kv_heads, common_values, head_dim)
    initial = (
        jnp.full((rows_here, kv_heads, common_values), masked_score, jnp.float32),
        jnp.zeros((rows_here, kv_heads, common_values), jnp.float32),
        jnp.zeros((rows_here, kv_heads, common_values, head_dim), jnp.float32),
    )
    running = initial
    k_piece = lax.all_gather(keys, "ctx", axis=0, tiled=True)
    v_piece = lax.all_gather(values, "ctx", axis=0, tiled=True)
    shard_count = k_piece.shape[0] // rows_here
    per_turn = 2
    turn_count = shard_count // per_turn
    k_pos = lookup_positions(span_order, jnp.int32(0), k_piece.shape[0], span_rows)
    k_steps = k_piece.reshape(turn_count, per_turn, rows_here, kv_heads, head_dim)
    v_steps = v_piece.reshape(turn_count, per_turn, rows_here, kv_heads, head_dim)
    p_steps = k_pos.reshape(turn_count, per_turn, rows_here)

    def one_turn(carried, inputs_now):
        partial_value, row_top, row_total = source_partials(
            q_local, own_pos, inputs_now[0], inputs_now[1], inputs_now[2], head_dim
        )
        for member in range(per_turn):
            carried = absorb(carried, partial_value[member], row_top[member], row_total[member])
        return (carried, None)

    running, unused = lax.scan(one_turn, running, (k_steps, v_steps, p_steps))
    merged = running[2] / running[1][..., None]
    return merged.reshape(rows_here, kv_heads * common_values * head_dim).astype(jnp.bfloat16)


def solution(mesh):
    return jax.shard_map(
        shards,
        mesh=mesh,
        in_specs=(
            P(("groups", "ctx"), ("head", "rep")),
            P(("groups", "ctx"), ("head", "rep")),
            P(("groups", "ctx"), ("head", "rep")),
            P(),
        ),
        out_specs=P(("groups", "ctx"), ("head", "rep")),
        check_vma=False,
    )
```

profile of v0, /device:TPU:0, one launch (start us, length us, event | category | flops | bytes accessed | tf_op | source)
XLA Modules:
  0.0 60.6 jit_solution(10825627206917604020)
XLA Ops:
  0.0 0.8 %select_reduce_fusion.1 = s32[256]{0:T(256)S(1)} fusion(s32[8]{0:T(128)} %param.9, s32[256]{0:T(256)S(1)} %and_select_fusion.2), kind=kLoop, calls=%fused_computation.45 | loop fusion | flops 5888 | bytes 2080 | tf_op jit(solution)/shard_map/reduce_sum | solution.py:15
  0.8 1.2 %copy.30 = bf16[256,1024]{0,1:T(8,128)(2,1)S(1)} copy(bf16[256,1024]{1,0:T(8,128)(2,1)} %param.6) | data formatting | bytes 1048576 | tf_op args[0]
  2.1 1.0 %copy.32 = bf16[256,2,4,128]{3,0,2,1:T(8,128)(2,1)} copy(bf16[256,2,4,128]{0,3,2,1:T(8,128)(2,1)S(1)} %bitcast.99) | data formatting | bytes 1048576
  3.1 17.6 %all_gather.6 = bf16[1024,256]{1,0:T(8,128)(2,1)S(1)} all-gather(bf16[256,256]{1,0:T(8,128)(2,1)} %param.7), channel_id=1, replica_groups=mesh['groups'=2,'ctx'=4,'head'=2,'rep'=2] {'ctx'}, dimensions={0}, use_global_device_ids=true | all-gather | bytes 655360 | tf_op jit(solution)/shard_map/all_gather | solution.py:69
  20.7 0.9 %reshape.66 = bf16[2,2,256,2,128]{4,3,2,1,0:T(2,128)(2,1)} reshape(bf16[1024,256]{1,0:T(8,128)(2,1)S(1)} %all_gather.6) | data formatting | bytes 1048576 | tf_op jit(solution)/shard_map/reshape | solution.py:75
  21.6 16.6 %all_gather.7 = bf16[1024,256]{1,0:T(8,128)(2,1)S(1)} all-gather(bf16[256,256]{1,0:T(8,128)(2,1)} %param.8), channel_id=1, replica_groups=mesh['groups'=2,'ctx'=4,'head'=2,'rep'=2] {'ctx'}, dimensions={0}, use_global_device_ids=true | all-gather | bytes 655360 | tf_op jit(solution)/shard_map/all_gather | solution.py:70
  38.2 0.9 %reshape.68 = bf16[2,2,256,2,128]{4,3,2,1,0:T(2,128)(2,1)} reshape(bf16[1024,256]{1,0:T(8,128)(2,1)S(1)} %all_gather.7) | data formatting | bytes 1048576 | tf_op jit(solution)/shard_map/reshape | solution.py:76
  39.3 20.2 %while.15 = (s32[]{:T(128)}, f32[256,2,4]{0,2,1:T(4,128)S(1)}, f32[256,2,4]{0,2,1:T(4,128)S(1)}, f32[256,2,4,128]{0,3,2,1:T(8,128)S(1)}, s32[2,2,256]{2,1,0:T(2,...) while((s32[]{:T(128)}, f32[256,2,4]{0,2,1:T(4,128)S(1)}, ...), condition=%wide.region_5.6_spmd.clone, body=%wide.region_2.5_spmd.clone.sunk | while | flops 549871616 | bytes 19995776 | solution.py:87
  39.3 1.4 %constant_dynamic-slice_fusion.3 = (bf16[1,2,256,2,128]{4,3,2,1,0:T(2,128)(2,1)S(1)}, bf16[1,2,256,2,128]{4,3,2,1,0:T(2,128)(2,1)S(1)}) fusion(bf16[2,2,256,2,128]{4,3,2,1,0:T(2,128)(2,1)} %get-tuple-element.251, s32[]{:T(128)} %get-tuple-element.232, bf16[2,2,256,2,128]{4,3,2,1,0:T(2,128)(2,1)} %get-tuple-element.249), kind=kLoop, calls=%fused_computation.38.clone.1 | loop fusion | bytes 1048580 | tf_op jit(solution)/shard_map/while/body/jit(dynamic_index_in_dim)/dynamic_slice | solution.py:87
  40.7 0.1 broadcast_compare_fusion.3
  40.8 1.9 %fusion.43 = (f32[2,256,2,4]{1,3,0,2:T(4,128)S(1)}, f32[2,2,256,256,4]{3,2,4,1,0:T(8,128)S(1)}) fusion(pred[2,256,256]{1,2,0:T(8,128)(4,1)S(1)} %broadcast_compare_fusion.3, bf16[256,2,4,128]{3,0,2,1:T(8,128)(2,1)} %get-tuple-element.250, bf16[1,2,256,2,128]{4,3,2,1,0:T(2,128)(2,1)S(1)} %get-tuple-element.209), kind=kOutput, calls=%fused_computation.2.clone.1 | convolution fusion | flops 271577088 | bytes 5128192 | tf_op jit(solution)/shard_map/while/body/eval_jaxpr/rhgd,cshd->crhgs/dot_general | solution.py:24
  42.7 1.2 %fusion.44 = (bf16[2,256,2,4,256]{1,4,3,0,2:T(8,128)(2,1)S(1)}, f32[2,256,2,4]{1,3,0,2:T(4,128)S(1)}) fusion(f32[2,2,256,256,4]{3,2,4,1,0:T(8,128)S(1)} %get-tuple-element.211, f32[2,256,2,4]{1,3,0,2:T(4,128)S(1)} %get-tuple-element.210, pred[2,256,256]{1,2,0:T(8,128)(4,1)S(1)} %broadcast_compare_fusion.3), kind=kLoop, calls=%fused_computation.3.clone.1 | loop fusion | flops 6287360 | bytes 6455296 | tf_op jit(solution)/shard_map/while/body/eval_jaxpr/convert_element_type | solution.py:34
  43.9 0.9 %copy.63 = bf16[1,2,256,2,128]{2,4,3,1,0:T(8,128)(2,1)} copy(bf16[1,2,256,2,128]{4,3,2,1,0:T(2,128)(2,1)S(1)} %get-tuple-element.216) | data formatting | bytes 524288 | tf_op jit(solution)/shard_map/while/body/jit(dynamic_index_in_dim)/dynamic_slice | solution.py:87
  44.8 2.4 %fusion.46 = bf16[2,256,2,4,128]{1,4,3,2,0:T(8,128)(2,1)} fusion(bf16[2,256,2,4,256]{1,4,3,0,2:T(8,128)(2,1)S(1)} %get-tuple-element.215, bf16[1,2,256,2,128]{2,4,3,1,0:T(8,128)(2,1)} %copy.63, f32[2,256,2,4]{1,3,0,2:T(4,128)S(1)} %get-tuple-element.212), kind=kOutput, calls=%fused_computation.6.clone.1 | convolution fusion | flops 269488128 | bytes 3424256 | tf_op jit(solution)/shard_map/while/body/eval_jaxpr/crhgs,cshd->crhgd/dot_general | solution.py:32
  47.2 2.1 %fusion.47 = f32[256,2,4,128]{0,3,2,1:T(8,128)S(1)} fusion(f32[256,2,4,128]{0,3,2,1:T(8,128)S(1)} %get-tuple-element.235, bf16[2,256,2,4,128]{1,4,3,2,0:T(8,128)(2,1)} %fusion.46, f32[256,2,4]{0,2,1:T(4,128)S(1)} %get-tuple-element.217, f32[256,2,4]{0,2,1:T(4,128)S(1)} %get-tuple-element.218, f32[256,2,4]{0,2,1:T(4,128)S(1)} %get-tuple-element.219, ...), kind=kLoop, calls=%fused_computation.10.clone.1 | loop fusion | flops 2359296 | bytes 3178497 | tf_op jit(solution)/shard_map/while/body/eval_jaxpr/add | solution.py:50
  49.4 1.4 %constant_dynamic-slice_fusion.3 = (bf16[1,2,256,2,128]{4,3,2,1,0:T(2,128)(2,1)S(1)}, bf16[1,2,256,2,128]{4,3,2,1,0:T(2,128)(2,1)S(1)}) fusion(bf16[2,2,256,2,128]{4,3,2,1,0:T(2,128)(2,1)} %get-tuple-element.251, s32[]{:T(128)} %get-tuple-element.232, bf16[2,2,256,2,128]{4,3,2,1,0:T(2,128)(2,1)} %get-tuple-element.249), kind=kLoop, calls=%fused_computation.38.clone.1 | loop fusion | bytes 1048580 | tf_op jit(solution)/shard_map/while/body/jit(dynamic_index_in_dim)/dynamic_slice | solution.py:87
  50.8 0.1 broadcast_compare_fusion.3
  50.9 1.9 %fusion.43 = (f32[2,256,2,4]{1,3,0,2:T(4,128)S(1)}, f32[2,2,256,256,4]{3,2,4,1,0:T(8,128)S(1)}) fusion(pred[2,256,256]{1,2,0:T(8,128)(4,1)S(1)} %broadcast_compare_fusion.3, bf16[256,2,4,128]{3,0,2,1:T(8,128)(2,1)} %get-tuple-element.250, bf16[1,2,256,2,128]{4,3,2,1,0:T(2,128)(2,1)S(1)} %get-tuple-element.209), kind=kOutput, calls=%fused_computation.2.clone.1 | convolution fusion | flops 271577088 | bytes 5128192 | tf_op jit(solution)/shard_map/while/body/eval_jaxpr/rhgd,cshd->crhgs/dot_general | solution.py:24
  52.8 1.2 %fusion.44 = (bf16[2,256,2,4,256]{1,4,3,0,2:T(8,128)(2,1)S(1)}, f32[2,256,2,4]{1,3,0,2:T(4,128)S(1)}) fusion(f32[2,2,256,256,4]{3,2,4,1,0:T(8,128)S(1)} %get-tuple-element.211, f32[2,256,2,4]{1,3,0,2:T(4,128)S(1)} %get-tuple-element.210, pred[2,256,256]{1,2,0:T(8,128)(4,1)S(1)} %broadcast_compare_fusion.3), kind=kLoop, calls=%fused_computation.3.clone.1 | loop fusion | flops 6287360 | bytes 6455296 | tf_op jit(solution)/shard_map/while/body/eval_jaxpr/convert_element_type | solution.py:34
  54.0 0.9 %copy.63 = bf16[1,2,256,2,128]{2,4,3,1,0:T(8,128)(2,1)} copy(bf16[1,2,256,2,128]{4,3,2,1,0:T(2,128)(2,1)S(1)} %get-tuple-element.216) | data formatting | bytes 524288 | tf_op jit(solution)/shard_map/while/body/jit(dynamic_index_in_dim)/dynamic_slice | solution.py:87
  54.9 2.4 %fusion.46 = bf16[2,256,2,4,128]{1,4,3,2,0:T(8,128)(2,1)} fusion(bf16[2,256,2,4,256]{1,4,3,0,2:T(8,128)(2,1)S(1)} %get-tuple-element.215, bf16[1,2,256,2,128]{2,4,3,1,0:T(8,128)(2,1)} %copy.63, f32[2,256,2,4]{1,3,0,2:T(4,128)S(1)} %get-tuple-element.212), kind=kOutput, calls=%fused_computation.6.clone.1 | convolution fusion | flops 269488128 | bytes 3424256 | tf_op jit(solution)/shard_map/while/body/eval_jaxpr/crhgs,cshd->crhgd/dot_general | solution.py:32
  57.3 2.1 %fusion.47 = f32[256,2,4,128]{0,3,2,1:T(8,128)S(1)} fusion(f32[256,2,4,128]{0,3,2,1:T(8,128)S(1)} %get-tuple-element.235, bf16[2,256,2,4,128]{1,4,3,2,0:T(8,128)(2,1)} %fusion.46, f32[256,2,4]{0,2,1:T(4,128)S(1)} %get-tuple-element.217, f32[256,2,4]{0,2,1:T(4,128)S(1)} %get-tuple-element.218, f32[256,2,4]{0,2,1:T(4,128)S(1)} %get-tuple-element.219, ...), kind=kLoop, calls=%fused_computation.10.clone.1 | loop fusion | flops 2359296 | bytes 3178497 | tf_op jit(solution)/shard_map/while/body/eval_jaxpr/add | solution.py:50
  59.5 0.1 divide_convert_fusion
  59.6 1.0 %copy.39 = bf16[256,1024]{1,0:T(8,128)(2,1)} copy(bf16[256,1024]{0,1:T(8,128)(2,1)S(1)} %bitcast.98) | data formatting | bytes 1048576 | tf_op jit(solution)/shard_map/convert_element_type | solution.py:89
  (16 shorter events, 0.2 us)
Async XLA Ops:
  0.0 39.1 %copy-start = (s32[8]{0:T(128)S(1)}, s32[8]{0:T(128)}, u32[]{:S(2)}) copy-start(s32[8]{0:T(128)} %param.9) | copy-start | bytes 100
where the time goes:
time: 61 us; the launch traced here: 60.6 us
  blocking collectives  34.1 us (56%)
  local copies, waits for them, and re-layouts  9.69 us (16%)
  matrix products  8.65 us (14%)
  other arithmetic  7.94 us (13%)
    all_gather x1, blocking collectives, shards(): k_piece = lax.all_gather(keys, 'ctx', axis=0, tiled=True)  17.6 us
    all_gather x1, blocking collectives, shards(): v_piece = lax.all_gather(values, 'ctx', axis=0, tiled=True)  16.6 us
    dot_general x2, matrix products, source_partials(): jnp.einsum('crhgs,cshd->crhgd', weights.astype(jnp.bfloat16), value_group...  4.85 us
    dynamic_slice x4, local copies, waits for them, and re-layouts, shards(): running, unused = lax.scan(one_turn, running, (k_steps, v_steps, p_steps))  4.53 us
    add x2, other arithmetic, absorb(): run_sum * rescale[..., None]  4.23 us
    dot_general x2, matrix products, source_partials(): jnp.einsum('rhgd,cshd->crhgs', query_block, key_group, preferred_element_...  3.8 us
    convert_element_type x2, other arithmetic, source_partials(): weights.astype(jnp.bfloat16)  2.34 us
    unnamed x4, local copies, waits for them, and re-layouts  2.27 us

commit v1 on v0

--- a/solution.py
+++ b/solution.py
@@ -66,7 +66,14 @@
         jnp.zeros((rows_here, kv_heads, common_values, head_dim), jnp.float32),
     )
     running = initial
-    k_piece = lax.all_gather(keys, "ctx", axis=0, tiled=True)
+    lanes = lax.axis_size("ctx")
+    all_blocks = [keys]
+    for pp in tuple(range(lanes - 1)):
+        o_now = lax.ppermute(all_blocks[-1], "ctx", [(m, (m + 1) % lanes) for m in range(lanes)])
+        all_blocks.append(o_now)
+    q_next = jnp.concatenate(all_blocks[::-1], axis=0)
+    opened = lax.axis_index("ctx")
+    k_piece = jnp.roll(q_next, (opened + 1) * keys.shape[0], axis=0)
     v_piece = lax.all_gather(values, "ctx", axis=0, tiled=True)
     shard_count = k_piece.shape[0] // rows_here
     per_turn = 2

time: 61 us -> 56.3 us (0.923)
  blocking collectives: 34.1 us -> 16.1 us
  waiting for transfers between devices: 0 us -> 9.49 us
  starting transfers between devices: 0 us -> 3.06 us
    all_gather x1 -> x0, blocking collectives: 17.6 us -> none  [shards(): k_piece = lax.all_gather(keys, 'ctx', axis=0, tiled=True)]
    ppermute x0 -> x3, waiting for transfers between devices: none -> 9.49 us  [shards(): lax.ppermute(all_blocks[-1], 'ctx', [(m, (m + 1) % lanes) for m in range(...]
    ppermute x0 -> x3, starting transfers between devices: none -> 3.06 us  [shards(): lax.ppermute(all_blocks[-1], 'ctx', [(m, (m + 1) % lanes) for m in range(...]
    unnamed x4 -> x11, local copies, waits for them, and re-layouts: 2.27 us -> 2.35 us
  transfers between devices with their start and end apart: 0 -> 3, of which waited for: 0 -> 2; matrix products, arithmetic and copies ran while one was open for 0% -> 8% of each run, Pallas kernels for 0% -> 0%
where the time goes in v1:
time: 56.3 us; the launch traced here: 55.9 us
  blocking collectives  16.1 us (29%)
  local copies, waits for them, and re-layouts  9.82 us (17%)
  waiting for transfers between devices  9.49 us (17%)
  matrix products  8.64 us (15%)
  other arithmetic  8.54 us (15%)
  starting transfers between devices  3.06 us (5%)
    all_gather x1, blocking collectives, shards(): v_piece = lax.all_gather(values, 'ctx', axis=0, tiled=True)  16.1 us
    ppermute x3, waiting for transfers between devices, shards(): lax.ppermute(all_blocks[-1], 'ctx', [(m, (m + 1) % lanes) for m in range(...  9.49 us
    dot_general x2, matrix products, source_partials(): jnp.einsum('crhgs,cshd->crhgd', weights.astype(jnp.bfloat16), value_group...  4.85 us
    dynamic_slice x4, local copies, waits for them, and re-layouts, shards(): running, unused = lax.scan(one_turn, running, (k_steps, v_steps, p_steps))  4.53 us
    add x2, other arithmetic, absorb(): run_sum * rescale[..., None]  4.23 us
    dot_general x2, matrix products, source_partials(): jnp.einsum('rhgd,cshd->crhgs', query_block, key_group, preferred_element_...  3.8 us
    ppermute x3, starting transfers between devices, shards(): lax.ppermute(all_blocks[-1], 'ctx', [(m, (m + 1) % lanes) for m in range(...  3.06 us
    unnamed x11, local copies, waits for them, and re-layouts  2.35 us
  transfers between devices with their start and end apart: 3, of which 2 were waited for; matrix products, arithmetic and copies ran while one was open for 8% of the time, Pallas kernels for 0%

profile of v1, /device:TPU:0, one launch (start us, length us, event | category | flops | bytes accessed | tf_op | source)
XLA Modules:
  0.0 55.9 jit_solution(14362548944117663367)
XLA Ops:
  0.0 3.1 %collective-permute-start = (bf16[256,256]{1,0:T(8,128)(2,1)}, bf16[256,256]{1,0:T(8,128)(2,1)S(1)}, u32[]{:S(2)}, u32[]{:S(2)}) collective-permute-start(bf16[256,256]{1,0:T(8,128)(2,1)} %param.7), channel_id=1, source_target_pairs={{0,4},{4,8},{8,12},{12,0},{1,5},{5,9},{9,13},{13,1},{2,6},{6,10},{... | collective-permute-start | bytes 393224 | tf_op jit(solution)/shard_map/ppermute | solution.py:72
  3.1 0.7 %select_reduce_fusion = s32[1024]{0:T(1024)S(1)} fusion(s32[8]{0:T(128)} %param.9, s32[1024]{0:T(1024)S(1)} %add_select_fusion), kind=kLoop, calls=%fused_computation.41 | loop fusion | flops 23552 | bytes 8224 | tf_op jit(solution)/shard_map/reduce_sum | solution.py:15
  3.8 16.1 %all_gather.3 = bf16[1024,256]{1,0:T(8,128)(2,1)S(1)} all-gather(bf16[256,256]{1,0:T(8,128)(2,1)} %param.8), channel_id=1, replica_groups=mesh['groups'=2,'ctx'=4,'head'=2,'rep'=2] {'ctx'}, dimensions={0}, use_global_device_ids=true | all-gather | bytes 655360 | tf_op jit(solution)/shard_map/all_gather | solution.py:77
  20.0 1.2 %copy.30 = bf16[256,1024]{0,1:T(8,128)(2,1)S(1)} copy(bf16[256,1024]{1,0:T(8,128)(2,1)} %param.6) | data formatting | bytes 1048576 | tf_op args[0]
  21.2 1.0 %copy.32 = bf16[256,2,4,128]{3,0,2,1:T(8,128)(2,1)} copy(bf16[256,2,4,128]{0,3,2,1:T(8,128)(2,1)S(1)} %bitcast.99) | data formatting | bytes 1048576
  22.3 0.9 %reshape.68 = bf16[2,2,256,2,128]{4,3,2,1,0:T(2,128)(2,1)} reshape(bf16[1024,256]{1,0:T(8,128)(2,1)S(1)} %all_gather.3) | data formatting | bytes 1048576 | tf_op jit(solution)/shard_map/reshape | solution.py:83
  23.2 0.7 %select_reduce_fusion.1 = s32[256]{0:T(256)S(1)} fusion(s32[8]{0:T(128)} %param.9, s32[256]{0:T(256)S(1)} %and_select_fusion.2), kind=kLoop, calls=%fused_computation.53 | loop fusion | flops 5888 | bytes 2080 | tf_op jit(solution)/shard_map/reduce_sum | solution.py:15
  23.9 2.7 %collective-permute-done.1 = bf16[256,256]{1,0:T(8,128)(2,1)S(1)} collective-permute-done((bf16[256,256]{1,0:T(8,128)(2,1)S(1)}, bf16[256,256]{1,0:T(8,128)(2,1)S(1)}, u32[]{:S(2)}, u32[]{:S(2)}) %collective-permute-start.1) | collective-permute-done | bytes 131104 | tf_op jit(solution)/shard_map/ppermute | solution.py:72
  26.7 6.8 %collective-permute-done.2 = bf16[256,256]{1,0:T(8,128)(2,1)S(1)} collective-permute-done((bf16[256,256]{1,0:T(8,128)(2,1)S(1)}, bf16[256,256]{1,0:T(8,128)(2,1)S(1)}, u32[]{:S(2)}, u32[]{:S(2)}) %collective-permute-start.2) | collective-permute-done | bytes 131104 | tf_op jit(solution)/shard_map/ppermute | solution.py:72
  33.6 0.9 %reshape.66 = bf16[2,2,256,2,128]{4,3,2,1,0:T(2,128)(2,1)} reshape(bf16[1024,256]{1,0:T(8,128)(2,1)S(1)} %constant_dynamic-slice_fusion.2) | data formatting | bytes 1048576 | tf_op jit(solution)/shard_map/reshape | solution.py:82
  34.6 20.2 %while.15 = (s32[]{:T(128)}, f32[256,2,4]{0,2,1:T(4,128)S(1)}, f32[256,2,4]{0,2,1:T(4,128)S(1)}, f32[256,2,4,128]{0,3,2,1:T(8,128)S(1)}, s32[2,2,256]{2,1,0:T(2,...) while((s32[]{:T(128)}, f32[256,2,4]{0,2,1:T(4,128)S(1)}, ...), condition=%wide.region_5.6_spmd.clone, body=%wide.region_2.5_spmd.clone.sunk | while | flops 549871616 | bytes 19995776 | solution.py:94
  34.6 1.4 %constant_dynamic-slice_fusion.4 = (bf16[1,2,256,2,128]{4,3,2,1,0:T(2,128)(2,1)S(1)}, bf16[1,2,256,2,128]{4,3,2,1,0:T(2,128)(2,1)S(1)}) fusion(bf16[2,2,256,2,128]{4,3,2,1,0:T(2,128)(2,1)} %get-tuple-element.251, s32[]{:T(128)} %get-tuple-element.232, bf16[2,2,256,2,128]{4,3,2,1,0:T(2,128)(2,1)} %get-tuple-element.249), kind=kLoop, calls=%fused_computation.38.clone.1 | loop fusion | bytes 1048580 | tf_op jit(solution)/shard_map/while/body/jit(dynamic_index_in_dim)/dynamic_slice | solution.py:94
  36.1 1.9 %fusion.43 = (f32[2,256,2,4]{1,3,0,2:T(4,128)S(1)}, f32[2,2,256,256,4]{3,2,4,1,0:T(8,128)S(1)}) fusion(pred[2,256,256]{1,2,0:T(8,128)(4,1)S(1)} %broadcast_compare_fusion.3, bf16[256,2,4,128]{3,0,2,1:T(8,128)(2,1)} %get-tuple-element.250, bf16[1,2,256,2,128]{4,3,2,1,0:T(2,128)(2,1)S(1)} %get-tuple-element.209), kind=kOutput, calls=%fused_computation.2.clone.1 | convolution fusion | flops 271577088 | bytes 5128192 | tf_op jit(solution)/shard_map/while/body/eval_jaxpr/rhgd,cshd->crhgs/dot_general | solution.py:24
  38.0 1.2 %fusion.44 = (bf16[2,256,2,4,256]{1,4,3,0,2:T(8,128)(2,1)S(1)}, f32[2,256,2,4]{1,3,0,2:T(4,128)S(1)}) fusion(f32[2,2,256,256,4]{3,2,4,1,0:T(8,128)S(1)} %get-tuple-element.211, f32[2,256,2,4]{1,3,0,2:T(4,128)S(1)} %get-tuple-element.210, pred[2,256,256]{1,2,0:T(8,128)(4,1)S(1)} %broadcast_compare_fusion.3), kind=kLoop, calls=%fused_computation.3.clone.1 | loop fusion | flops 6287360 | bytes 6455296 | tf_op jit(solution)/shard_map/while/body/eval_jaxpr/convert_element_type | solution.py:34
  39.2 0.9 %copy.63 = bf16[1,2,256,2,128]{2,4,3,1,0:T(8,128)(2,1)} copy(bf16[1,2,256,2,128]{4,3,2,1,0:T(2,128)(2,1)S(1)} %get-tuple-element.216) | data formatting | bytes 524288 | tf_op jit(solution)/shard_map/while/body/jit(dynamic_index_in_dim)/dynamic_slice | solution.py:94
  40.1 2.4 %fusion.46 = bf16[2,256,2,4,128]{1,4,3,2,0:T(8,128)(2,1)} fusion(bf16[2,256,2,4,256]{1,4,3,0,2:T(8,128)(2,1)S(1)} %get-tuple-element.215, bf16[1,2,256,2,128]{2,4,3,1,0:T(8,128)(2,1)} %copy.63, f32[2,256,2,4]{1,3,0,2:T(4,128)S(1)} %get-tuple-element.212), kind=kOutput, calls=%fused_computation.6.clone.1 | convolution fusion | flops 269488128 | bytes 3424256 | tf_op jit(solution)/shard_map/while/body/eval_jaxpr/crhgs,cshd->crhgd/dot_general | solution.py:32
  42.5 2.1 %fusion.47 = f32[256,2,4,128]{0,3,2,1:T(8,128)S(1)} fusion(f32[256,2,4,128]{0,3,2,1:T(8,128)S(1)} %get-tuple-element.235, bf16[2,256,2,4,128]{1,4,3,2,0:T(8,128)(2,1)} %fusion.46, f32[256,2,4]{0,2,1:T(4,128)S(1)} %get-tuple-element.217, f32[256,2,4]{0,2,1:T(4,128)S(1)} %get-tuple-element.218, f32[256,2,4]{0,2,1:T(4,128)S(1)} %get-tuple-element.219, ...), kind=kLoop, calls=%fused_computation.10.clone.1 | loop fusion | flops 2359296 | bytes 3178497 | tf_op jit(solution)/shard_map/while/body/eval_jaxpr/add | solution.py:50
  44.6 1.4 %constant_dynamic-slice_fusion.4 = (bf16[1,2,256,2,128]{4,3,2,1,0:T(2,128)(2,1)S(1)}, bf16[1,2,256,2,128]{4,3,2,1,0:T(2,128)(2,1)S(1)}) fusion(bf16[2,2,256,2,128]{4,3,2,1,0:T(2,128)(2,1)} %get-tuple-element.251, s32[]{:T(128)} %get-tuple-element.232, bf16[2,2,256,2,128]{4,3,2,1,0:T(2,128)(2,1)} %get-tuple-element.249), kind=kLoop, calls=%fused_computation.38.clone.1 | loop fusion | bytes 1048580 | tf_op jit(solution)/shard_map/while/body/jit(dynamic_index_in_dim)/dynamic_slice | solution.py:94
  46.2 1.9 %fusion.43 = (f32[2,256,2,4]{1,3,0,2:T(4,128)S(1)}, f32[2,2,256,256,4]{3,2,4,1,0:T(8,128)S(1)}) fusion(pred[2,256,256]{1,2,0:T(8,128)(4,1)S(1)} %broadcast_compare_fusion.3, bf16[256,2,4,128]{3,0,2,1:T(8,128)(2,1)} %get-tuple-element.250, bf16[1,2,256,2,128]{4,3,2,1,0:T(2,128)(2,1)S(1)} %get-tuple-element.209), kind=kOutput, calls=%fused_computation.2.clone.1 | convolution fusion | flops 271577088 | bytes 5128192 | tf_op jit(solution)/shard_map/while/body/eval_jaxpr/rhgd,cshd->crhgs/dot_general | solution.py:24
  48.1 1.2 %fusion.44 = (bf16[2,256,2,4,256]{1,4,3,0,2:T(8,128)(2,1)S(1)}, f32[2,256,2,4]{1,3,0,2:T(4,128)S(1)}) fusion(f32[2,2,256,256,4]{3,2,4,1,0:T(8,128)S(1)} %get-tuple-element.211, f32[2,256,2,4]{1,3,0,2:T(4,128)S(1)} %get-tuple-element.210, pred[2,256,256]{1,2,0:T(8,128)(4,1)S(1)} %broadcast_compare_fusion.3), kind=kLoop, calls=%fused_computation.3.clone.1 | loop fusion | flops 6287360 | bytes 6455296 | tf_op jit(solution)/shard_map/while/body/eval_jaxpr/convert_element_type | solution.py:34
  49.3 0.9 %copy.63 = bf16[1,2,256,2,128]{2,4,3,1,0:T(8,128)(2,1)} copy(bf16[1,2,256,2,128]{4,3,2,1,0:T(2,128)(2,1)S(1)} %get-tuple-element.216) | data formatting | bytes 524288 | tf_op jit(solution)/shard_map/while/body/jit(dynamic_index_in_dim)/dynamic_slice | solution.py:94
  50.2 2.4 %fusion.46 = bf16[2,256,2,4,128]{1,4,3,2,0:T(8,128)(2,1)} fusion(bf16[2,256,2,4,256]{1,4,3,0,2:T(8,128)(2,1)S(1)} %get-tuple-element.215, bf16[1,2,256,2,128]{2,4,3,1,0:T(8,128)(2,1)} %copy.63, f32[2,256,2,4]{1,3,0,2:T(4,128)S(1)} %get-tuple-element.212), kind=kOutput, calls=%fused_computation.6.clone.1 | convolution fusion | flops 269488128 | bytes 3424256 | tf_op jit(solution)/shard_map/while/body/eval_jaxpr/crhgs,cshd->crhgd/dot_general | solution.py:32
  52.6 2.1 %fusion.47 = f32[256,2,4,128]{0,3,2,1:T(8,128)S(1)} fusion(f32[256,2,4,128]{0,3,2,1:T(8,128)S(1)} %get-tuple-element.235, bf16[2,256,2,4,128]{1,4,3,2,0:T(8,128)(2,1)} %fusion.46, f32[256,2,4]{0,2,1:T(4,128)S(1)} %get-tuple-element.217, f32[256,2,4]{0,2,1:T(4,128)S(1)} %get-tuple-element.218, f32[256,2,4]{0,2,1:T(4,128)S(1)} %get-tuple-element.219, ...), kind=kLoop, calls=%fused_computation.10.clone.1 | loop fusion | flops 2359296 | bytes 3178497 | tf_op jit(solution)/shard_map/while/body/eval_jaxpr/add | solution.py:50
  54.9 1.0 %copy.39 = bf16[256,1024]{1,0:T(8,128)(2,1)} copy(bf16[256,1024]{0,1:T(8,128)(2,1)S(1)} %bitcast.98) | data formatting | bytes 1048576 | tf_op jit(solution)/shard_map/convert_element_type | solution.py:96
  (30 shorter events, 0.7 us)
Async XLA Ops:
  0.0 33.5 %copy-start = (bf16[256,256]{1,0:T(8,128)(2,1)S(1)}, bf16[256,256]{1,0:T(8,128)(2,1)}, u32[]{:S(2)}) copy-start(bf16[256,256]{1,0:T(8,128)(2,1)} %param.7) | copy-start | bytes 393220
  0.0 19.9 %collective-permute-start = (bf16[256,256]{1,0:T(8,128)(2,1)}, bf16[256,256]{1,0:T(8,128)(2,1)S(1)}, u32[]{:S(2)}, u32[]{:S(2)}) collective-permute-start(bf16[256,256]{1,0:T(8,128)(2,1)} %param.7), channel_id=1, source_target_pairs={{0,4},{4,8},{8,12},{12,0},{1,5},{5,9},{9,13},{13,1},{2,6},{6,10},{... | collective-permute-start | bytes 393224 | tf_op jit(solution)/shard_map/ppermute | solution.py:72
  19.9 6.8 %collective-permute-start.1 = (bf16[256,256]{1,0:T(8,128)(2,1)S(1)}, bf16[256,256]{1,0:T(8,128)(2,1)S(1)}, u32[]{:S(2)}, u32[]{:S(2)}) collective-permute-start(bf16[256,256]{1,0:T(8,128)(2,1)S(1)} %collective-permute-done), channel_id=1, source_target_pairs={{0,4},{4,8},{8,12},{12,0},{1,5},{5,9},{9,13},{13,1},{2,6},{6,10},{... | collective-permute-start | bytes 393224 | tf_op jit(solution)/shard_map/ppermute | solution.py:72
  26.7 6.8 %collective-permute-start.2 = (bf16[256,256]{1,0:T(8,128)(2,1)S(1)}, bf16[256,256]{1,0:T(8,128)(2,1)S(1)}, u32[]{:S(2)}, u32[]{:S(2)}) collective-permute-start(bf16[256,256]{1,0:T(8,128)(2,1)S(1)} %collective-permute-done.1), channel_id=1, source_target_pairs={{0,4},{4,8},{8,12},{12,0},{1,5},{5,9},{9,13},{13,1},{2,6},{6,10},{... | collective-permute-start | bytes 393224 | tf_op jit(solution)/shard_map/ppermute | solution.py:72
